TPU v7x, 256 devices: a whole 4x4x8 slice. The times are simulated.
256 devices in a mesh: band: 8 (over z_hi, y), grid: 32 (over z_lo, x, core).
Axes of the slice: x: 4, y: 4, z: 8 (z_hi: 2, z_lo: 4; z = z_hi * 4 + z_lo), core: 2. Of those that a mesh axis runs over, the one named last changes fastest.
Arguments:
- orbitals: bfloat16 [2048, 65536], P('band', 'grid'), as said below
- projectors: bfloat16 [2048, 65536], P('band', 'grid'), may hold values from -0.015625 to 0.015625
Outputs:
- result: bfloat16 [2048, 65536], P('band', 'grid')
- energies: float32 [2048], P('band')
Inputs may be any that keep to these rules, and one draw needn't show every extreme that they name: The orbitals are real-valued.
All inputs are finite; a program needn't handle non-finite values.
Results may differ from a plain program's by a relative error of at most 0.0049.
Values may be sent and summed in bfloat16 or wider, within the bound.
A program may use at most 64 MiB of HBM per device.

v0:
```python
import jax
import jax.numpy as jnp
from jax import lax
from jax.sharding import PartitionSpec as P


def split_up(array, dim, peers):
    lengths = array.shape
    blocks = array.reshape(*lengths[:dim], peers, lengths[dim] // peers, *lengths[dim + 1 :])
    return jnp.moveaxis(blocks, dim, 0)


def sum_at_owner(array, axis, dim):
    blocks = split_up(array, dim, lax.axis_size(axis))
    arrived = lax.all_to_all(blocks, axis, split_axis=0, concat_axis=0, tiled=True)
    return arrived.astype(jnp.float32).sum(axis=0)


def from_everyone(array, axis):
    peers = lax.axis_size(axis)
    return lax.all_to_all(
        jnp.broadcast_to(array[None], (peers, *array.shape)), axis, 0, 0, tiled=True
    )


def joined_along(blocks, dim):
    lengths = list(blocks.shape[1:])
    lengths[dim] *= blocks.shape[0]
    return jnp.moveaxis(blocks, 0, dim).reshape(lengths)


def gathered_copies(array, axis, dim):
    blocks = from_everyone(array, axis)
    return joined_along(blocks, dim)


def of_everyone(array, axis):
    everything = from_everyone(array, axis)
    return jnp.sum(everything, axis=0)


def together(arrays, axis):
    flat, at, done = (jnp.concatenate([a.reshape(-1) for a in arrays]), 0, [])
    subtotal = of_everyone(flat, axis)
    for a in arrays:
        done.append(subtotal[at : at + a.size].reshape(a.shape))
        at += a.size
    return tuple(done)


def local_intersection(rows, state):
    return lax.dot_general(
        rows, state, (((1,), (1,)), ((), ())), preferred_element_type=jnp.float32
    )


def local_apply(rounded, rows):
    return lax.dot_general(
        rounded, rows, (((0,), (0,)), ((), ())), preferred_element_type=jnp.float32
    )


def intersection_terms(state, whole):
    return local_intersection(whole, state)


def apply_terms(rounded, whole):
    return local_apply(rounded, whole)


def per_device(orbitals, projectors):
    total_bands = projectors.shape[0] * lax.axis_size("band")
    total_points = projectors.shape[1] * lax.axis_size("grid")
    whole = lax.all_gather(projectors, "band", axis=0, tiled=True)
    terms_first = intersection_terms(orbitals, whole)
    share_one = sum_at_owner(terms_first.astype(jnp.bfloat16), "grid", 0).astype(jnp.bfloat16)
    first_b = gathered_copies(share_one, "grid", 0)
    middle = (orbitals.astype(jnp.float32) - apply_terms(first_b, whole)).astype(jnp.bfloat16)
    widened = middle.astype(jnp.float32)
    local_norm = jnp.sum(widened * widened, axis=1)
    terms_second = intersection_terms(middle, whole)
    share_two = sum_at_owner(terms_second.astype(jnp.bfloat16), "grid", 0)
    share_b = share_two.astype(jnp.bfloat16)
    partial_value = jnp.sum(share_two * share_b.astype(jnp.float32), axis=0)
    intersection_numer, norm = together((partial_value, local_norm), "grid")
    second_b = gathered_copies(share_b, "grid", 0)
    change = apply_terms(second_b, whole)
    result = (widened - change).astype(jnp.bfloat16)
    numer = of_everyone(jnp.sum(widened * change, axis=1), "grid")
    energies = 2.0 * total_points / total_bands * numer / norm
    return (result, energies)


def solution(mesh):
    in_specs = (P("band", "grid"), P("band", "grid"))
    out_specs = (P("band", "grid"), P("band"))
    return jax.shard_map(
        per_device, mesh=mesh, in_specs=in_specs, out_specs=out_specs, check_vma=False
    )
```

profile of v0, /device:TPU:1, one launch (start us, length us, event | category | flops | bytes accessed | tf_op | source)
XLA Modules:
  0.0 369.0 jit_solution(16056781805258666253)
XLA Ops:
  7.2 0.0 all-gather.2.cloned.1.call-start
  7.2 0.7 all-gather.2.cloned.1.call-update
  7.9 0.0 copy-start
  7.9 178.6 %all-gather.2.cloned.1.call-done = bf16[2048,2048]{1,0:T(8,128)(2,1)} async-done(((bf16[256,2048]{1,0:T(8,128)(2,1)}), bf16[2048,2048]{1,0:T(8,128)(2,1)}) %all-gather.2.cloned.1.call-update) | async-done | bytes 8388624 | tf_op jit(solution)/shard_map/all_gather | solution.py:74
  186.6 6.0 %convolution_convert_fusion.1 = bf16[2048,256]{1,0:T(8,128)(2,1)S(1)} fusion(bf16[2048,2048]{1,0:T(8,128)(2,1)} %all-gather.2.cloned.1.call-done, bf16[256,2048]{1,0:T(8,128)(2,1)} %param.2), kind=kOutput, calls=%fused_computation.6 | convolution fusion | flops 2148007936 | bytes 10485760 | tf_op jit(solution)/shard_map/dot_general | solution.py:52
  192.6 32.3 %all_to_all.32 = bf16[32,64,256]{2,1,0:T(8,128)(2,1)S(1)} all-to-all(bf16[32,64,256]{2,1,0:T(8,128)(2,1)S(1)} %bitcast.19), channel_id=1, replica_groups=mesh['band'=8,'grid'=32] {'grid'}, dimensions={0} | all-to-all | bytes 2097152 | tf_op jit(solution)/shard_map/all_to_all | solution.py:15
  224.8 0.2 reduce_sum.66
  225.0 0.1 broadcast_in_dim.8
  225.1 31.6 %all_to_all.33 = bf16[32,64,256]{2,1,0:T(8,128)(2,1)S(1)} all-to-all(bf16[32,64,256]{2,1,0:T(8,128)(2,1)S(1)} %broadcast_in_dim.8), channel_id=1, replica_groups=mesh['band'=8,'grid'=32] {'grid'}, dimensions={0} | all-to-all | bytes 2097152 | tf_op jit(solution)/shard_map/all_to_all | solution.py:21
  256.7 0.0 slice-start
  256.7 0.0 copy-done
  256.7 0.0 slice-start.1
  256.7 5.9 %fusion = bf16[256,2048]{1,0:T(8,128)(2,1)S(1)} fusion(bf16[2048,256]{1,0:T(8,128)(2,1)S(1)} %bitcast.16, bf16[2048,2048]{1,0:T(8,128)(2,1)} %all-gather.2.cloned.1.call-done, bf16[256,2048]{1,0:T(8,128)(2,1)S(1)} %copy-done), kind=kOutput, calls=%fused_computation.4 | convolution fusion | flops 2149056512 | bytes 11534336 | tf_op jit(solution)/shard_map/dot_general | solution.py:58
  262.5 0.0 slice-done
  262.6 0.0 slice-done.1
  262.6 2.4 fusion.1
  264.9 0.5 copy.6
  265.5 31.6 %all_to_all.34 = bf16[32,64,256]{2,1,0:T(8,128)(2,1)S(1)} all-to-all(bf16[32,64,256]{2,1,0:T(8,128)(2,1)S(1)} %bitcast.17), channel_id=1, replica_groups=mesh['band'=8,'grid'=32] {'grid'}, dimensions={0} | all-to-all | bytes 2097152 | tf_op jit(solution)/shard_map/all_to_all | solution.py:15
  297.0 0.2 convert_reduce_fusion
  297.2 0.1 broadcast_in_dim.9
  297.3 31.6 %all_to_all.35 = bf16[32,64,256]{2,1,0:T(8,128)(2,1)S(1)} all-to-all(bf16[32,64,256]{2,1,0:T(8,128)(2,1)S(1)} %broadcast_in_dim.9), channel_id=1, replica_groups=mesh['band'=8,'grid'=32] {'grid'}, dimensions={0} | all-to-all | bytes 2097152 | tf_op jit(solution)/shard_map/all_to_all | solution.py:21
  328.9 6.8 %fusion.3 = (f32[256]{0:T(256)S(1)}, f32[256]{0:T(256)S(1)}, bf16[256,2048]{1,0:T(8,128)(2,1)}) fusion(bf16[256,2048]{1,0:T(8,128)(2,1)S(1)} %fusion, bf16[2048,256]{1,0:T(8,128)(2,1)S(1)} %bitcast.18, bf16[2048,2048]{1,0:T(8,128)(2,1)} %all-gather.2.cloned.1.call-done), kind=kOutput, calls=%fused_computation.9 | convolution fusion | flops 2151153152 | bytes 11536384 | tf_op jit(solution)/shard_map/dot_general | solution.py:58
  335.7 0.6 broadcast_in_dim.10
  336.3 5.1 %all-to-all-start.4 = ((f32[32,1,256]{2,1,0:T(1,128)}), f32[32,1,256]{2,1,0:T(1,128)S(1)}, u32[]{:S(2)}, u32[]{:S(2)}) async-start(f32[32,1,256]{2,1,0:T(1,128)} %broadcast_in_dim.10), calls=%async_computation.4 | async-start | bytes 65536 | tf_op jit(solution)/shard_map/all_to_all | solution.py:21
  341.5 7.6 %all-to-all-done.4 = f32[32,1,256]{2,1,0:T(1,128)S(1)} async-done(((f32[32,1,256]{2,1,0:T(1,128)}), f32[32,1,256]{2,1,0:T(1,128)S(1)}, u32[]{:S(2)}, u32[]{:S(2)}) %all-to-all-start.4) | async-done | bytes 32800 | tf_op jit(solution)/shard_map/all_to_all | solution.py:21
  349.1 0.7 broadcast_in_dim.11
  349.7 3.9 %all-to-all-start.5 = ((f32[32,1,512]{2,1,0:T(1,128)}), f32[32,1,512]{2,1,0:T(1,128)S(1)}, u32[]{:S(2)}, u32[]{:S(2)}) async-start(f32[32,1,512]{2,1,0:T(1,128)} %broadcast_in_dim.11), calls=%async_computation.5 | async-start | bytes 131072 | tf_op jit(solution)/shard_map/all_to_all | solution.py:21
  353.6 0.1 reduce_sum.69
  353.7 7.8 %all-to-all-done.5 = f32[32,1,512]{2,1,0:T(1,128)S(1)} async-done(((f32[32,1,512]{2,1,0:T(1,128)}), f32[32,1,512]{2,1,0:T(1,128)S(1)}, u32[]{:S(2)}, u32[]{:S(2)}) %all-to-all-start.5) | async-done | bytes 65568 | tf_op jit(solution)/shard_map/all_to_all | solution.py:21
  361.5 0.1 reduce_sum.72
  361.6 0.6 slice_divide_fusion
  (3 shorter events, 0.0 us)
Async XLA Ops:
  7.2 179.4 %all-gather.2.cloned.1.call-start = ((), (), s32[]{:S(2)}) async-start(), calls=%async_computation.6 | async-start | bytes 9437184 | tf_op jit(solution)/shard_map/all_gather | solution.py:74
  7.9 248.8 %copy-start = (bf16[256,2048]{1,0:T(8,128)(2,1)S(1)}, bf16[256,2048]{1,0:T(8,128)(2,1)}, u32[]{:S(2)}) copy-start(bf16[256,2048]{1,0:T(8,128)(2,1)} %param.2) | copy-start | bytes 3145732
  256.7 5.9 %slice-start = ((s8[8388608]{0:T(1024)(128)(4,1)}), s8[4194304]{0:T(1024)(128)(4,1)S(1)}, s32[]{:S(2)}) async-start(s8[8388608]{0:T(1024)(128)(4,1)} %bitcast.14), calls=%async_computation.7 | async-start | bytes 8388608
  256.7 5.9 %slice-start.1 = ((s8[8388608]{0:T(1024)(128)(4,1)}), s8[4194304]{0:T(1024)(128)(4,1)S(1)}, s32[]{:S(2)}) async-start(s8[8388608]{0:T(1024)(128)(4,1)} %bitcast.14), calls=%async_computation.8 | async-start | bytes 8388608
  336.3 12.7 %all-to-all-start.4 = ((f32[32,1,256]{2,1,0:T(1,128)}), f32[32,1,256]{2,1,0:T(1,128)S(1)}, u32[]{:S(2)}, u32[]{:S(2)}) async-start(f32[32,1,256]{2,1,0:T(1,128)} %broadcast_in_dim.10), calls=%async_computation.4 | async-start | bytes 65536 | tf_op jit(solution)/shard_map/all_to_all | solution.py:21
  349.7 11.8 %all-to-all-start.5 = ((f32[32,1,512]{2,1,0:T(1,128)}), f32[32,1,512]{2,1,0:T(1,128)S(1)}, u32[]{:S(2)}, u32[]{:S(2)}) async-start(f32[32,1,512]{2,1,0:T(1,128)} %broadcast_in_dim.11), calls=%async_computation.5 | async-start | bytes 131072 | tf_op jit(solution)/shard_map/all_to_all | solution.py:21
Sparse Core Ops, SparseCore 0:
  10.6 175.9 all-gather.1
where the time goes:
time: 369 us
  waiting for transfers between devices  195 us (53%)
  blocking collectives  127 us (34%)
  matrix products  21.1 us (6%)
  between operations  14.1 us (4%)
  starting transfers between devices  9.04 us (2%)
    all_gather x1, waiting for transfers between devices, per_device(): whole = lax.all_gather(projectors, 'band', axis=0, tiled=True)  179 us
    all_to_all x2, blocking collectives, sum_at_owner(): lax.all_to_all(blocks, axis, split_axis=0, concat_axis=0, tiled=True)  63.8 us
    all_to_all x2, blocking collectives, from_everyone(): lax.all_to_all(jnp.broadcast_to(array[None], (peers, *array.shape)), axis...  63.1 us
    all_to_all x2, waiting for transfers between devices, from_everyone(): lax.all_to_all(jnp.broadcast_to(array[None], (peers, *array.shape)), axis...  15.4 us
    dot_general x2, matrix products, local_apply(): lax.dot_general(rounded, rows, (((0,), (0,)), ((), ())), preferred_elemen...  12.7 us
    all_to_all x2, starting transfers between devices, from_everyone(): lax.all_to_all(jnp.broadcast_to(array[None], (peers, *array.shape)), axis...  9 us
    dot_general x2, matrix products, local_intersection(): lax.dot_general(rows, state, (((1,), (1,)), ((), ())), preferred_element_...  8.36 us
  transfers between devices with their start and end apart: 3, of which 3 were waited for; matrix products, arithmetic and copies ran while one was open for 0% of the time, Pallas kernels for 0%

commit v1 on v0

v1 whole, which is shorter than its diff:
```python
import functools

import jax
import jax.numpy as jnp
from jax import lax
from jax.experimental import pallas as pl
from jax.experimental.pallas import tpu as pltpu
from jax.sharding import PartitionSpec as P

MESH = pl.DeviceIdType.MESH
F32, BF16 = jnp.float32, jnp.bfloat16
NBLK = 8
CH = 4


def kernel(scale, psi_hbm, w_hbm, res, eout, wall, psi, psi1, acc, relay,
           xs, rc, xown, sx, bs, rx, sz, zs, rz, mbuf, mt, num, es, re,
           in_sem, w_send, yo, yf, zr, rl, zo, zf, s_send, s_recv, e_send, e_recv):
    rows, cols = psi.shape
    half = rows // 2
    crow = rows // CH
    b = lax.axis_index("band")
    g = lax.axis_index("grid")
    zh, y = b // 4, b % 4
    zl, x, c = g // 8, (g // 2) % 4, g % 2
    z = zh * 4 + zl

    def dev(zz, yy, xx, cc):
        return ((zz // 4) * 4 + yy, ((zz % 4) * 4 + xx) * 2 + cc)

    right, left = dev(z, (y + 1) % 4, x, c), dev(z, (y + 3) % 4, x, c)
    zup, zdn = dev((z + 2) % 8, y, x, c), dev((z + 6) % 8, y, x, c)
    mate = dev(z, y, x, 1 - c)
    xm = [(x + d) % 4 for d in (1, 2, 3)]
    zm = [(zl + d) % 4 for d in (1, 2, 3)]
    xdev = [dev(z, y, m, c) for m in xm]
    zdev = [dev(zh * 4 + m, y, x, c) for m in zm]

    def block(t):
        k = t % 4
        d = jnp.where(k == 1, 3, jnp.where(k == 2, 1, jnp.where(k == 3, 2, 0)))
        return ((zh + t // 4) % 2) * 4 + (y + d) % 4

    b_l, b_r, b_f = zh * 4 + (y + 3) % 4, zh * 4 + (y + 1) % 4, zh * 4 + (y + 2) % 4
    oz = 1 - zh
    z_o, z_l, z_r = oz * 4 + y, oz * 4 + (y + 3) % 4, oz * 4 + (y + 1) % 4
    z_f = oz * 4 + (y + 2) % 4

    def send(src, dst, ssem, rsem, to):
        pltpu.make_async_remote_copy(
            src_ref=src, dst_ref=dst, send_sem=ssem, recv_sem=rsem,
            device_id=to, device_id_type=MESH).start()

    def wait(ref, sem):
        pltpu.make_async_copy(ref, ref, sem).wait()

    def piece(blk, ch):
        return wall.at[blk, pl.ds(ch * crow, crow)]

    cw = pltpu.make_async_copy(w_hbm, wall.at[b], in_sem.at[0])
    cp = pltpu.make_async_copy(psi_hbm, psi, in_sem.at[1])
    cw.start()
    cp.start()

    barrier = pltpu.get_barrier_semaphore()
    peers = [right, left, zup, zdn, mate] + xdev + zdev
    for p in peers:
        pl.semaphore_signal(barrier, inc=1, device_id=p, device_id_type=MESH)
    acc[...] = jnp.zeros_like(acc)
    num[...] = jnp.zeros_like(num)
    es[...] = jnp.zeros_like(es)
    cw.wait()
    pl.semaphore_wait(barrier, len(peers))

    for cr, cl in ((0, 2), (1, 3), (2, 0), (3, 1)):
        send(piece(b, cr), piece(b, cr), w_send.at[0], yo.at[0, cr], right)
        send(piece(b, cl), piece(b, cl), w_send.at[0], yo.at[1, cl], left)
    for cu, cd in ((0, 2), (1, 3)):
        send(piece(b, cu), relay.at[cu], w_send.at[1], rl.at[cu], zup)
        send(piece(b, cd), relay.at[cd], w_send.at[1], rl.at[cd], zdn)
    cp.wait()

    def relay_on(ch):
        wait(relay.at[ch], rl.at[ch])
        if ch < 2:
            src = ((z + 6) % 8 // 4) * 4 + y
            send(relay.at[ch], piece(src, ch), w_send.at[2], zr.at[ch], zup)
        else:
            src = ((z + 2) % 8 // 4) * 4 + y
            send(relay.at[ch], piece(src, ch), w_send.at[2], zr.at[ch], zdn)

    def w_events(k):
        if k == 1:
            for cr, cl in ((0, 2), (1, 3)):
                wait(piece(b_l, cr), yo.at[0, cr])
                send(piece(b_l, cr), piece(b_l, cr), w_send.at[3], yf.at[cr], right)
                wait(piece(b_r, cl), yo.at[1, cl])
                send(piece(b_r, cl), piece(b_r, cl), w_send.at[3], yf.at[cl], left)
            relay_on(0)
            relay_on(2)
            wait(piece(b_l, 2), yo.at[0, 2])
            wait(piece(b_l, 3), yo.at[0, 3])
        elif k == 2:
            wait(piece(b_r, 0), yo.at[1, 0])
            wait(piece(b_r, 1), yo.at[1, 1])
            relay_on(1)
            relay_on(3)
        elif k == 3:
            wait(piece(b_f, 0), yf.at[0])
            wait(piece(b_f, 2), yf.at[2])
            for ch in (0, 2):
                wait(piece(z_o, ch), zr.at[ch])
                send(piece(z_o, ch), piece(z_o, ch), w_send.at[4], zo.at[0, ch], right)
                send(piece(z_o, ch), piece(z_o, ch), w_send.at[4], zo.at[1, ch], left)
            wait(piece(b_f, 1), yf.at[1])
            wait(piece(b_f, 3), yf.at[3])
        elif k == 4:
            for ch in (1, 3):
                wait(piece(z_o, ch), zr.at[ch])
                send(piece(z_o, ch), piece(z_o, ch), w_send.at[4], zo.at[0, ch], right)
                send(piece(z_o, ch), piece(z_o, ch), w_send.at[4], zo.at[1, ch], left)
        elif k == 5:
            for cr, cl in ((0, 2), (1, 3)):
                wait(piece(z_l, cr), zo.at[0, cr])
                send(piece(z_l, cr), piece(z_l, cr), w_send.at[5], zf.at[cr], right)
                wait(piece(z_r, cl), zo.at[1, cl])
                send(piece(z_r, cl), piece(z_r, cl), w_send.at[5], zf.at[cl], left)
            wait(piece(z_l, 2), zo.at[0, 2])
            wait(piece(z_l, 3), zo.at[0, 3])
        elif k == 6:
            wait(piece(z_r, 0), zo.at[1, 0])
            wait(piece(z_r, 1), zo.at[1, 1])
        elif k == 7:
            for ch in (0, 2, 1, 3):
                wait(piece(z_f, ch), zf.at[ch])

    def stage_a(p, t):
        state = psi if p == 0 else psi1
        v = lax.dot_general(wall[block(t)], state[...], (((1,), (1,)), ((), ())),
                            preferred_element_type=F32)
        lo, hi = v[:, :half], v[:, half:]
        xown[t] = jnp.where(c == 0, lo, hi)
        xs[p, t] = jnp.where(c == 0, hi, lo).astype(BF16)
        send(xs.at[p, t], rc.at[p, t], s_send.at[p, 0], s_recv.at[p, 0, t], mate)

    def stage_b(p, t):
        wait(rc.at[p, t], s_recv.at[p, 0, t])
        s = (xown[t] + rc[p, t].astype(F32)).reshape(4, rows // 4, half)
        bs[t] = s
        sx[p, t] = s.astype(BF16)
        for d in range(3):
            send(sx.at[p, t, xm[d]], rx.at[p, t, d], s_send.at[p, 1],
                 s_recv.at[p, 1, t], xdev[d])

    def stage_c(p, t):
        wait(rx.at[p, t], s_recv.at[p, 1, t])
        s = bs[t, x]
        for d in range(3):
            s = s + rx[p, t, d].astype(F32)
        s = s.reshape(4, rows // 16, half)
        zs[t] = s
        sz[p, t] = s.astype(BF16)
        for d in range(3):
            send(sz.at[p, t, zm[d]], rz.at[p, t, d], s_send.at[p, 2],
                 s_recv.at[p, 2, t], zdev[d])

    def stage_d(p, t):
        wait(rz.at[p, t], s_recv.at[p, 2, t])
        s = zs[t, zl]
        for d in range(3):
            s = s + rz[p, t, d].astype(F32)
        r = s.astype(BF16)
        mine = mbuf.at[p, c, block(t), x, zl]
        mine[...] = r
        if p == 1:
            num[...] += jnp.sum(s * r.astype(F32), axis=0, keepdims=True)
        for d in range(3):
            send(mine, mine, s_send.at[p, 3], s_recv.at[p, 3, t], zdev[d])

    def stage_e(p, t):
        wait(rz.at[p, t], s_recv.at[p, 3, t])
        mine = mbuf.at[p, c, block(t), x]
        for d in range(3):
            send(mine, mine, s_send.at[p, 4], s_recv.at[p, 4, t], xdev[d])

    def stage_f(p, t):
        wait(rx.at[p, t], s_recv.at[p, 4, t])
        mine = mbuf.at[p, c, block(t)]
        send(mine, mine, s_send.at[p, 5], s_recv.at[p, 5, t], mate)

    def stage_g(p, t):
        wait(rc.at[p, t], s_recv.at[p, 5, t])
        blk = block(t)
        for h in range(2):
            m = mbuf[p, h, blk].reshape(rows, half).astype(F32)
            mt[pl.ds(h * half, half), :] = m.T.astype(BF16)
        width = 512

        def part(i, carry):
            at = pl.ds(pl.multiple_of(i * width, width), width)
            acc[:, at] += jnp.dot(mt[...], wall[blk, :, at], preferred_element_type=F32)
            return carry

        lax.fori_loop(0, cols // width, part, 0)

    stages = (stage_a, stage_b, stage_c, stage_d, stage_e, stage_f, stage_g)

    def tick(T, carry):
        for k in range(1, 7):
            @pl.when(T == k)
            def _(k=k):
                w_events(k)

        for s in (6, 5, 4, 3, 2, 1):
            u = T - s

            @pl.when(((u >= 0) & (u <= 6)) | (u == 10))
            def _(s=s, u=u):
                stages[s](0, jnp.minimum(u, 7))

        @pl.when(T == 10)
        def _():
            w_events(7)

        @pl.when((T <= 6) | (T == 10))
        def _():
            stage_a(0, jnp.minimum(T, 7))

        return carry

    lax.fori_loop(0, 17, tick, 0)

    step = 64

    def first(i, carry):
        at = pl.ds(pl.multiple_of(i * step, step), step)
        v = (psi[at, :].astype(F32) - acc[at, :]).astype(BF16)
        psi1[at, :] = v
        acc[at, :] = jnp.zeros((step, cols), F32)
        w = v.astype(F32)
        n = jnp.sum(w * w, axis=1, keepdims=True)
        mtn = jnp.broadcast_to(n, (step, half))
        xown[0, at, :] = mtn
        return carry

    lax.fori_loop(0, rows // step, first, 0)
    for h in range(2):
        es[0, pl.ds(1 + h, 1), :] = xown[0, pl.ds(h * half, half), :].T[0:1, :]

    def run(s):
        def body(t, carry):
            stages[s](1, t)
            return carry

        lax.fori_loop(0, NBLK, body, 0)

    for s in range(4):
        run(s)
    es[0, 0:1, :] = num[...]
    for d in range(3):
        send(es.at[0], re.at[0, d], e_send.at[0], e_recv.at[0], zdev[d])
    run(4)
    wait(re.at[0], e_recv.at[0])
    es[1] = es[0] + re[0, 0] + re[0, 1] + re[0, 2]
    for d in range(3):
        send(es.at[1], re.at[1, d], e_send.at[1], e_recv.at[1], xdev[d])
    run(5)
    wait(re.at[1], e_recv.at[1])
    es[2] = es[1] + re[1, 0] + re[1, 1] + re[1, 2]
    send(es.at[2], re.at[2, 0], e_send.at[2], e_recv.at[2], mate)
    run(6)

    def last(i, carry):
        at = pl.ds(pl.multiple_of(i * step, step), step)
        res[at, :] = (psi1[at, :].astype(F32) - acc[at, :]).astype(BF16)
        return carry

    lax.fori_loop(0, rows // step, last, 0)

    wait(re.at[2, 0], e_recv.at[2])
    own, other = es[2, 0:1, :], re[2, 0, 0:1, :]
    lo = jnp.where(c == 0, own, other)
    hi = jnp.where(c == 0, other, own)
    norm = es[2, 1:3, :] + re[2, 0, 1:3, :]
    eout[0:1, :] = scale * lo / norm[0:1]
    eout[1:2, :] = scale * hi / norm[1:2]

    wait(wall.at[pl.ds(0, 2)], w_send.at[0])
    wait(wall.at[0], w_send.at[1])
    wait(wall.at[0], w_send.at[2])
    wait(wall.at[0], w_send.at[3])
    wait(wall.at[pl.ds(0, 2)], w_send.at[4])
    wait(wall.at[0], w_send.at[5])
    for p in range(2):
        for k, ref in enumerate((rc, rx, rz, rz, rx, rc)):
            wait(ref.at[p], s_send.at[p, k])
    wait(re.at[0], e_send.at[0])
    wait(re.at[1], e_send.at[1])
    wait(re.at[2, 0], e_send.at[2])


def per_device(orbitals, projectors):
    rows, cols = orbitals.shape
    half, crow = rows // 2, rows // CH
    bands = rows * lax.axis_size("band")
    points = cols * lax.axis_size("grid")
    dma = pltpu.SemaphoreType.DMA
    vmem = pltpu.VMEM
    result, energies = pl.pallas_call(
        functools.partial(kernel, 2.0 * points / bands),
        out_shape=(jax.ShapeDtypeStruct((rows, cols), BF16),
                   jax.ShapeDtypeStruct((2, half), F32)),
        in_specs=[pl.BlockSpec(memory_space=pl.ANY)] * 2,
        out_specs=(pl.BlockSpec(memory_space=pltpu.VMEM),
                   pl.BlockSpec(memory_space=pltpu.VMEM)),
        scratch_shapes=[
            vmem((NBLK, rows, cols), BF16),
            vmem((rows, cols), BF16),
            vmem((rows, cols), BF16),
            vmem((rows, cols), F32),
            vmem((CH, crow, cols), BF16),
            vmem((2, NBLK, rows, half), BF16),
            vmem((2, NBLK, rows, half), BF16),
            vmem((NBLK, rows, half), F32),
            vmem((2, NBLK, 4, rows // 4, half), BF16),
            vmem((NBLK, 4, rows // 4, half), F32),
            vmem((2, NBLK, 3, rows // 4, half), BF16),
            vmem((2, NBLK, 4, rows // 16, half), BF16),
            vmem((NBLK, 4, rows // 16, half), F32),
            vmem((2, NBLK, 3, rows // 16, half), BF16),
            vmem((2, 2, NBLK, 4, 4, rows // 16, half), BF16),
            vmem((rows, rows), BF16),
            vmem((1, half), F32),
            vmem((3, 8, half), F32),
            vmem((3, 3, 8, half), F32),
            dma((2,)),
            dma((6,)),
            dma((2, CH)),
            dma((CH,)),
            dma((CH,)),
            dma((CH,)),
            dma((2, CH)),
            dma((CH,)),
            dma((2, 6)),
            dma((2, 6, NBLK)),
            dma((3,)),
            dma((3,)),
        ],
        compiler_params=pltpu.CompilerParams(
            collective_id=0, has_side_effects=True, vmem_limit_bytes=60_000_000),
    )(orbitals, projectors)
    return result, energies.reshape(rows)


def solution(mesh):
    in_specs = (P("band", "grid"), P("band", "grid"))
    out_specs = (P("band", "grid"), P("band"))
    return jax.shard_map(
        per_device, mesh=mesh, in_specs=in_specs, out_specs=out_specs, check_vma=False
    )
```

time: 369 us -> 155 us (0.42)
  waiting for transfers between devices: 195 us -> 0 us
  Pallas kernels: 0 us -> 151 us
  blocking collectives: 127 us -> 0 us
  matrix products: 21.1 us -> 0 us
  between operations: 14.1 us -> 0.65 us
  starting transfers between devices: 9.04 us -> 0 us
    all_gather x1 -> x0, waiting for transfers between devices: 179 us -> none  [per_device(): whole = lax.all_gather(projectors, 'band', axis=0, tiled=True)]
    pallas_call x0 -> x1, Pallas kernels: none -> 151 us  [per_device(): pl.pallas_call(functools.partial(kernel, 2.0 * points / bands), out_shape...]
    all_to_all x4 -> x0, blocking collectives: 127 us -> none  [the longest x2 63.8 us: sum_at_owner(): lax.all_to_all(blocks, axis, split_axis=0, concat_axis=0, tiled=True)]
    dot_general x4 -> x0, matrix products: 21.1 us -> none  [the longest x2 12.7 us: local_apply(): lax.dot_general(rounded, rows, (((0,), (0,)), ((), ())), preferred_elemen...]
    all_to_all x2 -> x0, waiting for transfers between devices: 15.4 us -> none  [from_everyone(): lax.all_to_all(jnp.broadcast_to(array[None], (peers, *array.shape)), axis...]
    all_to_all x2 -> x0, starting transfers between devices: 9 us -> none  [from_everyone(): lax.all_to_all(jnp.broadcast_to(array[None], (peers, *array.shape)), axis...]
  transfers between devices with their start and end apart: 3 -> 0, of which waited for: 3 -> 0; matrix products, arithmetic and copies ran while one was open for 0% -> 0% of each run, Pallas kernels for 0% -> 0%
where the time goes in v1:
time: 155 us
  Pallas kernels  151 us (97%)
  local copies, waits for them, and re-layouts  2.87 us (2%)
    pallas_call x1, Pallas kernels, per_device(): pl.pallas_call(functools.partial(kernel, 2.0 * points / bands), out_shape...  151 us

profile of v1, /device:TPU:1, one launch (start us, length us, event | category | flops | bytes accessed | tf_op | source)
XLA Modules:
  0.0 154.6 jit_solution(6709316570642740240)
XLA Ops:
  0.6 151.0 %shard_map.41 = (bf16[256,2048]{1,0:T(8,128)(2,1)}, f32[2,128]{1,0:T(2,128)}) custom-call(bf16[256,2048]{1,0:T(8,128)(2,1)} %psi_hbm.1, bf16[256,2048]{1,0:T(8,128)(2,1)} %w_hbm.1), custom_call_target="tpu_custom_call" | custom-call | tf_op jit(solution)/shard_map/pallas_call | solution.py:309
  151.7 0.0 copy-start
  151.7 2.3 %copy.6 = bf16[256,2048]{1,0:T(8,128)(2,1)} copy(bf16[256,2048]{1,0:T(8,128)(2,1)} %get-tuple-element.8) | data formatting | bytes 2097152
  154.0 0.0 copy-done
  154.0 0.6 copy.7
Async XLA Ops:
  151.7 2.3 %copy-start = (f32[2,128]{1,0:T(2,128)S(1)}, f32[2,128]{1,0:T(2,128)}, u32[]{:S(2)}) copy-start(f32[2,128]{1,0:T(2,128)} %get-tuple-element.5) | copy-start | bytes 3076

commit v2 on v0

v2 whole, which is shorter than its diff:
```python
import functools

import jax
import jax.numpy as jnp
from jax import lax
from jax.experimental import pallas as pl
from jax.experimental.pallas import tpu as pltpu
from jax.sharding import PartitionSpec as P

MESH = pl.DeviceIdType.MESH
F32, BF16 = jnp.float32, jnp.bfloat16
CH = 4
NU = 8
NT = (((1,), (1,)), ((), ()))


def kernel(scale, psi_hbm, w_hbm, res, eout, wall, st, psi1, acc,
           xs, rc, xown, sx, bs, rx, sz, zs, rz, m1f, mbuf, sg, mt, mt2, nrm, es, re,
           in_sem, w_send, n_recv, f_recv, z_recv, s_send, c_recv, x_recv, zz_recv,
           gz_recv, gx_recv, gc_recv, sr_recv, sc_recv, hz_recv, hx_recv, hc_recv,
           e_send, e_recv):
    rows, cols = psi1.shape
    half = rows // 2
    crow = rows // CH
    b = lax.axis_index("band")
    g = lax.axis_index("grid")
    zh, y = b // 4, b % 4
    zl, x, c = g // 8, (g // 2) % 4, g % 2

    def dev(hh, yy, ll, xx, cc):
        return (hh * 4 + yy, (ll * 4 + xx) * 2 + cc)

    ym = [(y + d) % 4 for d in (1, 3, 2)]
    xm = [(x + d) % 4 for d in (1, 2, 3)]
    zm = [(zl + d) % 4 for d in (1, 2, 3)]
    ydev = [dev(zh, m, zl, x, c) for m in ym]
    odev = [dev(1 - zh, m, zl, x, c) for m in ym]
    right, left = ydev[0], ydev[1]
    zpart = dev(1 - zh, y, zl, x, c)
    mate = dev(zh, y, zl, x, 1 - c)
    xdev = [dev(zh, y, zl, m, c) for m in xm]
    zdev = [dev(zh, y, m, x, c) for m in zm]

    def unit(t):
        return (t % 4) * 2 + (zh + t // 4) % 2

    def send(src, dst, ssem, rsem, to):
        pltpu.make_async_remote_copy(
            src_ref=src, dst_ref=dst, send_sem=ssem, recv_sem=rsem,
            device_id=to, device_id_type=MESH).start()

    def wait(ref, sem):
        pltpu.make_async_copy(ref, ref, sem).wait()

    own = [wall.at[ch * 2 + zh, y] for ch in range(CH)]
    loads = [pltpu.make_async_copy(w_hbm.at[pl.ds(ch * crow, crow)], own[ch], in_sem.at[ch])
             for ch in range(CH)]
    loads.append(pltpu.make_async_copy(psi_hbm, st.at[pl.ds(0, rows)], in_sem.at[CH]))
    loads.append(pltpu.make_async_copy(w_hbm, st.at[pl.ds(rows, rows)], in_sem.at[CH + 1]))
    for load in loads:
        load.start()

    barrier = pltpu.get_barrier_semaphore()
    peers = ydev + odev + [zpart, mate] + xdev + zdev
    for p in peers:
        pl.semaphore_signal(barrier, inc=1, device_id=p, device_id_type=MESH)
    acc[...] = jnp.zeros_like(acc)
    es[...] = jnp.zeros_like(es)
    for load in loads:
        load.wait()
    pl.semaphore_wait(barrier, len(peers))

    for ch in range(CH):
        send(own[ch], own[ch], w_send.at[1], z_recv.at[ch], zpart)

    def near(k):
        piece = wall.at[unit(k), y]
        send(piece, piece, w_send.at[0], n_recv.at[0, k], right)
        send(piece, piece, w_send.at[0], n_recv.at[1, k], left)

    near(0)
    near(1)

    def pass_on(k):
        for side, m, to in ((0, (y + 3) % 4, right), (1, (y + 1) % 4, left)):
            wait(wall.at[0, 0], n_recv.at[side, k])
            part = wall.at[unit(k), m, pl.ds(side * (crow // 2), crow // 2)]
            send(part, part, w_send.at[2], f_recv.at[k], to)

        @pl.when((k + 2 >= CH) & (k + 2 < NU))
        def _():
            wait(wall.at[0, 0], z_recv.at[k + 2 - CH])

        @pl.when(k + 2 < NU)
        def _():
            near(k + 2)

    def stage_a(t):
        v = lax.dot_general(wall[unit(t)].reshape(rows, cols), st[...], NT,
                            preferred_element_type=F32)
        q = [v[:, i * half:(i + 1) * half] for i in range(4)]
        for i in range(2):
            at = slice(i * half, (i + 1) * half)
            xown[:, at] = jnp.where(c == 0, q[2 * i], q[2 * i + 1])
            xs[t, :, at] = jnp.where(c == 0, q[2 * i + 1], q[2 * i]).astype(BF16)
        send(xs.at[t], rc.at[t], s_send.at[0], c_recv.at[t], mate)

    def stage_b(t):
        wait(rc.at[t], c_recv.at[t])
        s = (xown[...] + rc[t].astype(F32)).reshape(4, crow, rows)
        bs[...] = s
        sx[t] = s.astype(BF16)
        for d in range(3):
            send(sx.at[t, xm[d]], rx.at[t, d], s_send.at[1], x_recv.at[t], xdev[d])

    def stage_c(t):
        wait(rx.at[t], x_recv.at[t])
        s = bs[x]
        for d in range(3):
            s = s + rx[t, d].astype(F32)
        s = s.reshape(4, crow // 4, rows)
        zs[t] = s
        sz[t] = s.astype(BF16)
        for d in range(3):
            send(sz.at[t, zm[d]], rz.at[t, d], s_send.at[2], zz_recv.at[t], zdev[d])

    def stage_d(t):
        wait(rz.at[t], zz_recv.at[t])
        s = zs[t, zl]
        for d in range(3):
            s = s + rz[t, d].astype(F32)
        u = unit(t)
        m1f[u] = s[:, :half]
        mine, mys = mbuf.at[0, c, u, x, zl], sg.at[c, u, b]
        mine[...] = s[:, :half].astype(BF16)
        mys[...] = s[:, half:].astype(BF16)
        for d in range(3):
            send(mine, mine, s_send.at[3], gz_recv.at[t], zdev[d])
        for to in odev + [zpart] + ydev:
            send(mys, mys, s_send.at[6], sr_recv.at[u], to)

    def stage_e(t):
        wait(mbuf.at[0, 0, 0, 0, pl.ds(0, 3)], gz_recv.at[t])
        mine = mbuf.at[0, c, unit(t), x]
        for d in range(3):
            send(mine, mine, s_send.at[4], gx_recv.at[t], xdev[d])

    def stage_f(t):
        wait(mbuf.at[0, 0, 0, pl.ds(0, 3)], gx_recv.at[t])
        mine = mbuf.at[0, c, unit(t)]
        send(mine, mine, s_send.at[5], gc_recv.at[t], mate)

    width = 512

    def stage_g(t):
        wait(mbuf.at[0, 0, 0], gc_recv.at[t])
        u = unit(t)
        for h in range(2):
            m = mbuf[0, h, u].reshape(rows, half).astype(F32)
            mt[pl.ds(h * half, half), :] = m.T.astype(BF16)

        def part(i, carry):
            at = pl.ds(pl.multiple_of(i * width, width), width)
            acc[:, at] += jnp.dot(mt[...], wall[u, :, :, at].reshape(rows, width),
                                  preferred_element_type=F32)
            return carry

        lax.fori_loop(0, cols // width, part, 0)

    late = 5

    def done(t):
        return jnp.where(t < late, 0, t - 1)

    def over(stage, lo, hi):
        def body(t, carry):
            stage(t)
            return carry

        lax.fori_loop(lo, hi, body, 0)

    def tick(n, carry):
        @pl.when(n < NU)
        def _():
            pass_on(n)

        t = n - 1
        two, one, now = done(t - 2), done(t - 1), done(t)

        @pl.when(t >= 1)
        def _():
            stage_c(t - 1)

        over(stage_d, one, now)
        over(stage_f, two, one)

        @pl.when(t >= 0)
        def _():
            wait(wall.at[0, 0], f_recv.at[t])
            stage_a(t)

        @pl.when(t >= 0)
        def _():
            stage_b(t)

        over(stage_e, one, now)
        over(stage_g, jnp.where(t == NU - 2, 0, 2), 2)
        return carry

    lax.fori_loop(0, NU + 1, tick, 0)
    stage_d(NU - 2)
    over(stage_g, 2, 4)
    stage_c(NU - 1)
    stage_f(NU - 3)
    stage_e(NU - 2)
    over(stage_g, 4, 6)
    stage_d(NU - 1)
    early = NU - 2
    for u in range(early):
        wait(sg.at[0, 0, pl.ds(0, 7)], sr_recv.at[u])
    send(sg.at[c, pl.ds(0, early)], sg.at[c, pl.ds(0, early)], s_send.at[7], sc_recv.at[0], mate)
    stage_f(NU - 2)
    stage_g(NU - 2)
    stage_e(NU - 1)
    for u in range(early, NU):
        wait(sg.at[0, 0, pl.ds(0, 7)], sr_recv.at[u])
    send(sg.at[c, pl.ds(early, 2)], sg.at[c, pl.ds(early, 2)], s_send.at[7], sc_recv.at[1], mate)
    stage_f(NU - 1)
    wait(sg.at[0, pl.ds(0, early)], sc_recv.at[0])
    wait(sg.at[0, pl.ds(0, 2)], sc_recv.at[1])

    m2 = m1f[...].reshape(NU * crow // 4, half)
    for o in range(8):
        for h in range(2):
            k = [mbuf[0, c, (2 * h + i) * 2 + o // 4, o % 4].reshape(crow, half)
                 for i in range(2)]
            m2 = m2 - jnp.dot(sg[h, :, o].reshape(NU * crow // 4, half),
                              jnp.concatenate(k, axis=0), preferred_element_type=F32)
    r = m2.astype(BF16)
    es[0, 0:1, :] = jnp.sum(m2 * r.astype(F32), axis=0, keepdims=True)
    share = crow // 4
    for u in range(NU):
        mbuf[1, c, u, x, zl] = r[u * share:(u + 1) * share]
    NP = 4
    for p in range(NP):
        mine = mbuf.at[1, c, pl.ds(2 * p, 2), x, zl]
        for d in range(3):
            send(mine, mine, s_send.at[8], hz_recv.at[p], zdev[d])

    stage_g(NU - 1)
    step = 64

    def first(i, carry):
        at = pl.ds(pl.multiple_of(i * step, step), step)
        v = (st[at, :].astype(F32) - acc[at, :]).astype(BF16)
        psi1[at, :] = v
        w = v.astype(F32)
        n = jnp.sum(w * w, axis=1, keepdims=True)
        nrm[at, :] = jnp.broadcast_to(n, (step, half))
        return carry

    lax.fori_loop(0, rows // step, first, 0)
    for h in range(2):
        es[0, pl.ds(1 + h, 1), :] = nrm[pl.ds(h * half, half), :].T[0:1, :]
    for d in range(3):
        send(es.at[0], re.at[0, d], e_send.at[0], e_recv.at[0], zdev[d])
    for p in range(NP):
        wait(mbuf.at[0, 0, pl.ds(0, 2), 0, pl.ds(0, 3)], hz_recv.at[p])
        mine = mbuf.at[1, c, pl.ds(2 * p, 2), x]
        for d in range(3):
            send(mine, mine, s_send.at[9], hx_recv.at[p], xdev[d])
    wait(re.at[0], e_recv.at[0])
    es[1] = es[0] + re[0, 0] + re[0, 1] + re[0, 2]
    for d in range(3):
        send(es.at[1], re.at[1, d], e_send.at[1], e_recv.at[1], xdev[d])

    def turn(p, h):
        for u in (2 * p, 2 * p + 1):
            m = mbuf[1, h, u].reshape(rows, half).astype(F32)
            mt2[pl.ds(pl.multiple_of(h * half, half), half), u * rows:(u + 1) * rows] = (
                m.T.astype(BF16))

    for p in range(NP):
        wait(mbuf.at[0, 0, pl.ds(0, 2), pl.ds(0, 3)], hx_recv.at[p])
        mine = mbuf.at[1, c, pl.ds(2 * p, 2)]
        send(mine, mine, s_send.at[10], hc_recv.at[p], mate)
        turn(p, c)
    wait(re.at[1], e_recv.at[1])
    es[2] = es[1] + re[1, 0] + re[1, 1] + re[1, 2]
    send(es.at[2], re.at[2, 0], e_send.at[2], e_recv.at[2], mate)
    for p in range(NP):
        wait(mbuf.at[0, 0, pl.ds(0, 2)], hc_recv.at[p])
        turn(p, 1 - c)

    def last(i, carry):
        at = pl.ds(pl.multiple_of(i * width, width), width)
        change = jnp.dot(mt2[...], wall[:, :, :, at].reshape(NU * rows, width),
                         preferred_element_type=F32)
        res[:, at] = (psi1[:, at].astype(F32) - change).astype(BF16)
        return carry

    lax.fori_loop(0, cols // width, last, 0)

    wait(re.at[2, 0], e_recv.at[2])
    mine, other = es[2, 0:1, :], re[2, 0, 0:1, :]
    norm = es[2, 1:3, :] + re[2, 0, 1:3, :]
    eout[0:1, :] = scale * jnp.where(c == 0, mine, other) / norm[0:1]
    eout[1:2, :] = scale * jnp.where(c == 0, other, mine) / norm[1:2]

    wait(wall.at[pl.ds(0, 4)], w_send.at[0])
    wait(wall.at[0], w_send.at[1])
    wait(wall.at[pl.ds(0, 2)], w_send.at[2])
    sizes = (rc, rx, rz, mbuf.at[0, 0, :, 0, pl.ds(0, 3)], mbuf.at[0, 0, :, pl.ds(0, 3)],
             mbuf.at[0, 0], sg.at[0, :, pl.ds(0, 7)], sg.at[0],
             mbuf.at[0, 0, :, 0, pl.ds(0, 3)], mbuf.at[0, 0, :, pl.ds(0, 3)], mbuf.at[0, 0])
    for k, ref in enumerate(sizes):
        wait(ref, s_send.at[k])
    wait(re.at[0], e_send.at[0])
    wait(re.at[1], e_send.at[1])
    wait(re.at[2, 0], e_send.at[2])


def per_device(orbitals, projectors):
    rows, cols = orbitals.shape
    half, crow = rows // 2, rows // CH
    share = crow // 4
    bands = rows * lax.axis_size("band")
    points = cols * lax.axis_size("grid")
    dma = pltpu.SemaphoreType.DMA
    vmem = pltpu.VMEM
    result, energies = pl.pallas_call(
        functools.partial(kernel, 2.0 * points / bands),
        out_shape=(jax.ShapeDtypeStruct((rows, cols), BF16),
                   jax.ShapeDtypeStruct((2, half), F32)),
        in_specs=[pl.BlockSpec(memory_space=pl.ANY)] * 2,
        out_specs=(pl.BlockSpec(memory_space=pltpu.VMEM),
                   pl.BlockSpec(memory_space=pltpu.VMEM)),
        scratch_shapes=[
            vmem((NU, 4, crow, cols), BF16),
            vmem((2 * rows, cols), BF16),
            vmem((rows, cols), BF16),
            vmem((rows, cols), F32),
            vmem((NU, rows, rows), BF16),
            vmem((NU, rows, rows), BF16),
            vmem((rows, rows), F32),
            vmem((NU, 4, crow, rows), BF16),
            vmem((4, crow, rows), F32),
            vmem((NU, 3, crow, rows), BF16),
            vmem((NU, 4, share, rows), BF16),
            vmem((NU, 4, share, rows), F32),
            vmem((NU, 3, share, rows), BF16),
            vmem((NU, share, half), F32),
            vmem((2, 2, NU, 4, 4, share, half), BF16),
            vmem((2, NU, 8, share, half), BF16),
            vmem((rows, rows), BF16),
            vmem((rows, NU * rows), BF16),
            vmem((rows, half), F32),
            vmem((3, 8, half), F32),
            vmem((3, 3, 8, half), F32),
            dma((CH + 2,)),
            dma((3,)),
            dma((2, NU)),
            dma((NU,)),
            dma((CH,)),
            dma((11,)),
            dma((NU,)),
            dma((NU,)),
            dma((NU,)),
            dma((NU,)),
            dma((NU,)),
            dma((NU,)),
            dma((NU,)),
            dma((2,)),
            dma((4,)),
            dma((4,)),
            dma((4,)),
            dma((3,)),
            dma((3,)),
        ],
        compiler_params=pltpu.CompilerParams(
            collective_id=0, has_side_effects=True, vmem_limit_bytes=60_000_000),
    )(orbitals, projectors)
    return result, energies.reshape(rows)


def solution(mesh):
    in_specs = (P("band", "grid"), P("band", "grid"))
    out_specs = (P("band", "grid"), P("band"))
    return jax.shard_map(
        per_device, mesh=mesh, in_specs=in_specs, out_specs=out_specs, check_vma=False
    )
```

time: 369 us -> 124 us (0.34)
  waiting for transfers between devices: 195 us -> 0 us
  blocking collectives: 127 us -> 0 us
  Pallas kernels: 0 us -> 121 us
  matrix products: 21.1 us -> 0 us
  between operations: 14.1 us -> 0.65 us
  starting transfers between devices: 9.04 us -> 0 us
    all_gather x1 -> x0, waiting for transfers between devices: 179 us -> none  [per_device(): whole = lax.all_gather(projectors, 'band', axis=0, tiled=True)]
    all_to_all x4 -> x0, blocking collectives: 127 us -> none  [the longest x2 63.8 us: sum_at_owner(): lax.all_to_all(blocks, axis, split_axis=0, concat_axis=0, tiled=True)]
    pallas_call x0 -> x1, Pallas kernels: none -> 121 us  [per_device(): pl.pallas_call(functools.partial(kernel, 2.0 * points / bands), out_shape...]
    dot_general x4 -> x0, matrix products: 21.1 us -> none  [the longest x2 12.7 us: local_apply(): lax.dot_general(rounded, rows, (((0,), (0,)), ((), ())), preferred_elemen...]
    all_to_all x2 -> x0, waiting for transfers between devices: 15.4 us -> none  [from_everyone(): lax.all_to_all(jnp.broadcast_to(array[None], (peers, *array.shape)), axis...]
    all_to_all x2 -> x0, starting transfers between devices: 9 us -> none  [from_everyone(): lax.all_to_all(jnp.broadcast_to(array[None], (peers, *array.shape)), axis...]
  transfers between devices with their start and end apart: 3 -> 0, of which waited for: 3 -> 0; matrix products, arithmetic and copies ran while one was open for 0% -> 0% of each run, Pallas kernels for 0% -> 0%
where the time goes in v2:
time: 124 us
  Pallas kernels  121 us (98%)
  local copies, waits for them, and re-layouts  2.87 us (2%)
    pallas_call x1, Pallas kernels, per_device(): pl.pallas_call(functools.partial(kernel, 2.0 * points / bands), out_shape...  121 us
    unnamed x4, local copies, waits for them, and re-layouts  2.87 us

profile of v2, /device:TPU:1, one launch (start us, length us, event | category | flops | bytes accessed | tf_op | source)
XLA Modules:
  0.0 124.3 jit_solution(1523634833008873272)
XLA Ops:
  0.6 120.8 %shard_map.41 = (bf16[256,2048]{1,0:T(8,128)(2,1)}, f32[2,128]{1,0:T(2,128)}) custom-call(bf16[256,2048]{1,0:T(8,128)(2,1)} %psi_hbm.1, bf16[256,2048]{1,0:T(8,128)(2,1)} %w_hbm.1), custom_call_target="tpu_custom_call" | custom-call | tf_op jit(solution)/shard_map/pallas_call | solution.py:331
  121.4 0.0 copy-start
  121.4 2.3 %copy.6 = bf16[256,2048]{1,0:T(8,128)(2,1)} copy(bf16[256,2048]{1,0:T(8,128)(2,1)} %get-tuple-element.8) | data formatting | bytes 2097152
  123.7 0.0 copy-done
  123.7 0.6 copy.7
Async XLA Ops:
  121.4 2.3 %copy-start = (f32[2,128]{1,0:T(2,128)S(1)}, f32[2,128]{1,0:T(2,128)}, u32[]{:S(2)}) copy-start(f32[2,128]{1,0:T(2,128)} %get-tuple-element.5) | copy-start | bytes 3076

commit v3 on v2

--- a/solution.py
+++ b/solution.py
@@ -16,7 +16,7 @@
 
 def kernel(scale, psi_hbm, w_hbm, res, eout, wall, st, psi1, acc,
            xs, rc, xown, sx, bs, rx, sz, zs, rz, m1f, mbuf, sg, mt, mt2, nrm, es, re,
-           in_sem, w_send, n_recv, f_recv, z_recv, s_send, c_recv, x_recv, zz_recv,
+           in_sem, w_send, n_recv, m_recv, f_recv, z_recv, s_send, c_recv, x_recv, zz_recv,
            gz_recv, gx_recv, gc_recv, sr_recv, sc_recv, hz_recv, hx_recv, hc_recv,
            e_send, e_recv):
     rows, cols = psi1.shape
@@ -52,6 +52,10 @@
     def wait(ref, sem):
         pltpu.make_async_copy(ref, ref, sem).wait()
 
+    barrier = pltpu.get_barrier_semaphore()
+    peers = odev + [zpart] + zdev + ydev + xdev + [mate]
+    for p in peers:
+        pl.semaphore_signal(barrier, inc=1, device_id=p, device_id_type=MESH)
     own = [wall.at[ch * 2 + zh, y] for ch in range(CH)]
     loads = [pltpu.make_async_copy(w_hbm.at[pl.ds(ch * crow, crow)], own[ch], in_sem.at[ch])
              for ch in range(CH)]
@@ -59,41 +63,46 @@
     loads.append(pltpu.make_async_copy(w_hbm, st.at[pl.ds(rows, rows)], in_sem.at[CH + 1]))
     for load in loads:
         load.start()
-
-    barrier = pltpu.get_barrier_semaphore()
-    peers = ydev + odev + [zpart, mate] + xdev + zdev
-    for p in peers:
-        pl.semaphore_signal(barrier, inc=1, device_id=p, device_id_type=MESH)
+    for load in loads[:CH]:
+        load.wait()
+    pl.semaphore_wait(barrier, len(peers))
+
+    for ch in range(CH):
+        send(own[ch], own[ch], w_send.at[1], z_recv.at[ch], zpart)
+
+    hrow = crow // 2
+
+    def near(k, kept):
+        for side, to in ((0, right), (1, left)):
+            part = wall.at[unit(k), y, pl.ds((side ^ kept) * hrow, hrow)]
+            sem = m_recv.at[k] if kept else n_recv.at[side, k]
+            send(part, part, w_send.at[0], sem, to)
+
+    def pass_on(k):
+        for side, m, to in ((0, (y + 3) % 4, right), (1, (y + 1) % 4, left)):
+            wait(wall.at[0, 0, pl.ds(0, hrow)], n_recv.at[side, k])
+            part = wall.at[unit(k), m, pl.ds(side * hrow, hrow)]
+            send(part, part, w_send.at[2], f_recv.at[k], to)
+
+        @pl.when(k + 1 < NU)
+        def _():
+            near(k + 1, 1)
+
+        @pl.when((k + 2 >= CH) & (k + 2 < NU))
+        def _():
+            wait(wall.at[0, 0], z_recv.at[k + 2 - CH])
+
+        @pl.when(k + 2 < NU)
+        def _():
+            near(k + 2, 0)
+
+    near(0, 0)
+    near(0, 1)
+    near(1, 0)
     acc[...] = jnp.zeros_like(acc)
     es[...] = jnp.zeros_like(es)
-    for load in loads:
+    for load in loads[CH:]:
         load.wait()
-    pl.semaphore_wait(barrier, len(peers))
-
-    for ch in range(CH):
-        send(own[ch], own[ch], w_send.at[1], z_recv.at[ch], zpart)
-
-    def near(k):
-        piece = wall.at[unit(k), y]
-        send(piece, piece, w_send.at[0], n_recv.at[0, k], right)
-        send(piece, piece, w_send.at[0], n_recv.at[1, k], left)
-
-    near(0)
-    near(1)
-
-    def pass_on(k):
-        for side, m, to in ((0, (y + 3) % 4, right), (1, (y + 1) % 4, left)):
-            wait(wall.at[0, 0], n_recv.at[side, k])
-            part = wall.at[unit(k), m, pl.ds(side * (crow // 2), crow // 2)]
-            send(part, part, w_send.at[2], f_recv.at[k], to)
-
-        @pl.when((k + 2 >= CH) & (k + 2 < NU))
-        def _():
-            wait(wall.at[0, 0], z_recv.at[k + 2 - CH])
-
-        @pl.when(k + 2 < NU)
-        def _():
-            near(k + 2)
 
     def stage_a(t):
         v = lax.dot_general(wall[unit(t)].reshape(rows, cols), st[...], NT,
@@ -108,14 +117,14 @@
     def stage_b(t):
         wait(rc.at[t], c_recv.at[t])
         s = (xown[...] + rc[t].astype(F32)).reshape(4, crow, rows)
-        bs[...] = s
+        bs[t % 2] = s
         sx[t] = s.astype(BF16)
         for d in range(3):
             send(sx.at[t, xm[d]], rx.at[t, d], s_send.at[1], x_recv.at[t], xdev[d])
 
     def stage_c(t):
         wait(rx.at[t], x_recv.at[t])
-        s = bs[x]
+        s = bs[t % 2, x]
         for d in range(3):
             s = s + rx[t, d].astype(F32)
         s = s.reshape(4, crow // 4, rows)
@@ -167,7 +176,7 @@
 
         lax.fori_loop(0, cols // width, part, 0)
 
-    late = 5
+    late = 4
 
     def done(t):
         return jnp.where(t < late, 0, t - 1)
@@ -185,17 +194,10 @@
             pass_on(n)
 
         t = n - 1
-        two, one, now = done(t - 2), done(t - 1), done(t)
-
-        @pl.when(t >= 1)
-        def _():
-            stage_c(t - 1)
-
-        over(stage_d, one, now)
-        over(stage_f, two, one)
 
         @pl.when(t >= 0)
         def _():
+            wait(wall.at[0, 0], m_recv.at[t])
             wait(wall.at[0, 0], f_recv.at[t])
             stage_a(t)
 
@@ -203,28 +205,39 @@
         def _():
             stage_b(t)
 
-        over(stage_e, one, now)
-        over(stage_g, jnp.where(t == NU - 2, 0, 2), 2)
+        @pl.when(t >= 1)
+        def _():
+            stage_c(t - 1)
+
+        over(stage_d, done(t - 1), done(t))
+        over(stage_e, done(t - 2), done(t - 1))
+        over(stage_f, done(t - 3), done(t - 2))
         return carry
 
     lax.fori_loop(0, NU + 1, tick, 0)
+    stage_g(0)
+    stage_c(NU - 1)
+    stage_e(NU - 3)
+    stage_f(NU - 4)
+    stage_g(1)
     stage_d(NU - 2)
-    over(stage_g, 2, 4)
-    stage_c(NU - 1)
+    stage_g(2)
+    stage_d(NU - 1)
     stage_f(NU - 3)
+    stage_g(3)
     stage_e(NU - 2)
-    over(stage_g, 4, 6)
-    stage_d(NU - 1)
     early = NU - 2
     for u in range(early):
         wait(sg.at[0, 0, pl.ds(0, 7)], sr_recv.at[u])
     send(sg.at[c, pl.ds(0, early)], sg.at[c, pl.ds(0, early)], s_send.at[7], sc_recv.at[0], mate)
+    stage_g(4)
+    stage_e(NU - 1)
     stage_f(NU - 2)
-    stage_g(NU - 2)
-    stage_e(NU - 1)
+    stage_g(5)
     for u in range(early, NU):
         wait(sg.at[0, 0, pl.ds(0, 7)], sr_recv.at[u])
     send(sg.at[c, pl.ds(early, 2)], sg.at[c, pl.ds(early, 2)], s_send.at[7], sc_recv.at[1], mate)
+    stage_g(6)
     stage_f(NU - 1)
     wait(sg.at[0, pl.ds(0, early)], sc_recv.at[0])
     wait(sg.at[0, pl.ds(0, 2)], sc_recv.at[1])
@@ -242,10 +255,19 @@
     for u in range(NU):
         mbuf[1, c, u, x, zl] = r[u * share:(u + 1) * share]
     NP = 4
+
+    def leg(p, k):
+        at = pl.ds(2 * p, 2)
+        if k == 0:
+            return mbuf.at[1, c, at, x, zl], (zdev if p < NP - 1 else xdev)
+        if p < NP - 1:
+            return mbuf.at[1, c, at, x], xdev
+        return mbuf.at[1, c, at, :, zl], zdev
+
     for p in range(NP):
-        mine = mbuf.at[1, c, pl.ds(2 * p, 2), x, zl]
-        for d in range(3):
-            send(mine, mine, s_send.at[8], hz_recv.at[p], zdev[d])
+        mine, to = leg(p, 0)
+        for d in range(3):
+            send(mine, mine, s_send.at[8], hz_recv.at[p], to[d])
 
     stage_g(NU - 1)
     step = 64
@@ -266,9 +288,9 @@
         send(es.at[0], re.at[0, d], e_send.at[0], e_recv.at[0], zdev[d])
     for p in range(NP):
         wait(mbuf.at[0, 0, pl.ds(0, 2), 0, pl.ds(0, 3)], hz_recv.at[p])
-        mine = mbuf.at[1, c, pl.ds(2 * p, 2), x]
-        for d in range(3):
-            send(mine, mine, s_send.at[9], hx_recv.at[p], xdev[d])
+        mine, to = leg(p, 1)
+        for d in range(3):
+            send(mine, mine, s_send.at[9], hx_recv.at[p], to[d])
     wait(re.at[0], e_recv.at[0])
     es[1] = es[0] + re[0, 0] + re[0, 1] + re[0, 2]
     for d in range(3):
@@ -330,8 +352,8 @@
     vmem = pltpu.VMEM
     result, energies = pl.pallas_call(
         functools.partial(kernel, 2.0 * points / bands),
-        out_shape=(jax.ShapeDtypeStruct((rows, cols), BF16),
-                   jax.ShapeDtypeStruct((2, half), F32)),
+        out_shape=(pltpu.VMEM((rows, cols), BF16),
+                   pltpu.VMEM((2, half), F32)),
         in_specs=[pl.BlockSpec(memory_space=pl.ANY)] * 2,
         out_specs=(pl.BlockSpec(memory_space=pltpu.VMEM),
                    pl.BlockSpec(memory_space=pltpu.VMEM)),
@@ -344,7 +366,7 @@
             vmem((NU, rows, rows), BF16),
             vmem((rows, rows), F32),
             vmem((NU, 4, crow, rows), BF16),
-            vmem((4, crow, rows), F32),
+            vmem((2, 4, crow, rows), F32),
             vmem((NU, 3, crow, rows), BF16),
             vmem((NU, 4, share, rows), BF16),
             vmem((NU, 4, share, rows), F32),
@@ -361,6 +383,7 @@
             dma((3,)),
             dma((2, NU)),
             dma((NU,)),
+            dma((NU,)),
             dma((CH,)),
             dma((11,)),
             dma((NU,)),
@@ -378,7 +401,7 @@
             dma((3,)),
         ],
         compiler_params=pltpu.CompilerParams(
-            collective_id=0, has_side_effects=True, vmem_limit_bytes=60_000_000),
+            collective_id=0, has_side_effects=True, vmem_limit_bytes=65_500_000),
     )(orbitals, projectors)
     return result, energies.reshape(rows)
 

time: 124 us -> 117 us (0.944)
  Pallas kernels: 121 us -> 115 us
  local copies, waits for them, and re-layouts: 2.87 us -> 1.54 us
    pallas_call x1, Pallas kernels: 121 us -> 115 us  [per_device(): pl.pallas_call(functools.partial(kernel, 2.0 * points / bands), out_shape...]
    unnamed x4 -> x2, local copies, waits for them, and re-layouts: 2.87 us -> 1.54 us
where the time goes in v3:
time: 117 us
  Pallas kernels  115 us (98%)
  local copies, waits for them, and re-layouts  1.54 us (1%)
    pallas_call x1, Pallas kernels, per_device(): pl.pallas_call(functools.partial(kernel, 2.0 * points / bands), out_shape...  115 us

profile of v3, /device:TPU:1, one launch (start us, length us, event | category | flops | bytes accessed | tf_op | source)
XLA Modules:
  0.0 116.8 jit_solution(6212010059768142151)
XLA Ops:
  0.6 114.6 %shard_map.41 = (bf16[256,2048]{1,0:T(8,128)(2,1)S(1)}, f32[2,128]{1,0:T(2,128)S(1)}) custom-call(bf16[256,2048]{1,0:T(8,128)(2,1)} %psi_hbm.1, bf16[256,2048]{1,0:T(8,128)(2,1)} %w_hbm.1), custom_call_target="tpu_custom_call" | custom-call | tf_op jit(solution)/shard_map/pallas_call | solution.py:353
  115.3 1.0 copy.6
  116.2 0.6 copy.7

commit v4 on v3

--- a/solution.py
+++ b/solution.py
@@ -31,8 +31,8 @@
         return (hh * 4 + yy, (ll * 4 + xx) * 2 + cc)
 
     ym = [(y + d) % 4 for d in (1, 3, 2)]
-    xm = [(x + d) % 4 for d in (1, 2, 3)]
-    zm = [(zl + d) % 4 for d in (1, 2, 3)]
+    xm = [(x + d) % 4 for d in (2, 1, 3)]
+    zm = [(zl + d) % 4 for d in (2, 1, 3)]
     ydev = [dev(zh, m, zl, x, c) for m in ym]
     odev = [dev(1 - zh, m, zl, x, c) for m in ym]
     right, left = ydev[0], ydev[1]
@@ -40,6 +40,9 @@
     mate = dev(zh, y, zl, x, 1 - c)
     xdev = [dev(zh, y, zl, m, c) for m in xm]
     zdev = [dev(zh, y, m, x, c) for m in zm]
+    cross = [dev(zh, y, m, n, c) for m in zm for n in xm]
+    bcore = [dev(1 - zh, m, zl, x, 1 - c) for m in ym + [y]] + [
+        dev(zh, m, zl, x, 1 - c) for m in ym]
 
     def unit(t):
         return (t % 4) * 2 + (zh + t // 4) % 2
@@ -53,7 +56,7 @@
         pltpu.make_async_copy(ref, ref, sem).wait()
 
     barrier = pltpu.get_barrier_semaphore()
-    peers = odev + [zpart] + zdev + ydev + xdev + [mate]
+    peers = odev + [zpart] + bcore + cross + zdev + ydev + xdev + [mate]
     for p in peers:
         pl.semaphore_signal(barrier, inc=1, device_id=p, device_id_type=MESH)
     own = [wall.at[ch * 2 + zh, y] for ch in range(CH)]
@@ -140,13 +143,30 @@
             s = s + rz[t, d].astype(F32)
         u = unit(t)
         m1f[u] = s[:, :half]
-        mine, mys = mbuf.at[0, c, u, x, zl], sg.at[c, u, b]
+        mine = mbuf.at[0, c, u, x, zl]
         mine[...] = s[:, :half].astype(BF16)
-        mys[...] = s[:, half:].astype(BF16)
-        for d in range(3):
-            send(mine, mine, s_send.at[3], gz_recv.at[t], zdev[d])
+        sg[c, u, b] = s[:, half:].astype(BF16)
+        last_unit = isinstance(t, int) and t == NU - 1
+        if last_unit:
+            spread(t)
+        for to in cross + zdev + xdev if last_unit else zdev:
+            send(mine, mine, s_send.at[12 if last_unit else 3], gz_recv.at[t], to)
+
+    def spread(t):
+        u = unit(t)
+        mys = sg.at[c, u, b]
         for to in odev + [zpart] + ydev:
             send(mys, mys, s_send.at[6], sr_recv.at[u], to)
+
+        def both_cores():
+            for to in bcore + [mate]:
+                send(mys, mys, s_send.at[11], sr_recv.at[u], to)
+
+        if isinstance(t, int):
+            if t % CH == CH - 1:
+                both_cores()
+        else:
+            pl.when(t % CH == CH - 1)(both_cores)
 
     def stage_e(t):
         wait(mbuf.at[0, 0, 0, 0, pl.ds(0, 3)], gz_recv.at[t])
@@ -210,6 +230,7 @@
             stage_c(t - 1)
 
         over(stage_d, done(t - 1), done(t))
+        over(spread, done(t - 1), done(t))
         over(stage_e, done(t - 2), done(t - 1))
         over(stage_f, done(t - 3), done(t - 2))
         return carry
@@ -221,6 +242,7 @@
     stage_f(NU - 4)
     stage_g(1)
     stage_d(NU - 2)
+    spread(NU - 2)
     stage_g(2)
     stage_d(NU - 1)
     stage_f(NU - 3)
@@ -231,16 +253,13 @@
         wait(sg.at[0, 0, pl.ds(0, 7)], sr_recv.at[u])
     send(sg.at[c, pl.ds(0, early)], sg.at[c, pl.ds(0, early)], s_send.at[7], sc_recv.at[0], mate)
     stage_g(4)
-    stage_e(NU - 1)
+    stage_g(5)
+    fifteen = mbuf.at[0, 0, pl.ds(0, 5), pl.ds(0, 3), 0]
     stage_f(NU - 2)
-    stage_g(5)
+    wait(sg.at[0, pl.ds(0, early)], sc_recv.at[0])
+    wait(fifteen, gz_recv.at[NU - 1])
     for u in range(early, NU):
-        wait(sg.at[0, 0, pl.ds(0, 7)], sr_recv.at[u])
-    send(sg.at[c, pl.ds(early, 2)], sg.at[c, pl.ds(early, 2)], s_send.at[7], sc_recv.at[1], mate)
-    stage_g(6)
-    stage_f(NU - 1)
-    wait(sg.at[0, pl.ds(0, early)], sc_recv.at[0])
-    wait(sg.at[0, pl.ds(0, 2)], sc_recv.at[1])
+        wait(fifteen, sr_recv.at[u])
 
     m2 = m1f[...].reshape(NU * crow // 4, half)
     for o in range(8):
@@ -258,17 +277,30 @@
 
     def leg(p, k):
         at = pl.ds(2 * p, 2)
-        if k == 0:
-            return mbuf.at[1, c, at, x, zl], (zdev if p < NP - 1 else xdev)
+        mine = [mbuf.at[1, c, at, x, zl]]
         if p < NP - 1:
-            return mbuf.at[1, c, at, x], xdev
-        return mbuf.at[1, c, at, :, zl], zdev
+            first, then = zdev, xdev
+            others = [mbuf.at[1, c, at, x, m] for m in zm]
+        else:
+            first, then = xdev, zdev
+            others = [mbuf.at[1, c, at, m, zl] for m in xm]
+        return ((mine, first, 8, hz_recv), (mine, then, 9, hx_recv),
+                (others, then, 9, hx_recv))[k]
+
+    def go(p, k):
+        parts, to, ssem, rsem = leg(p, k)
+        for part in parts:
+            for d in range(3):
+                send(part, part, s_send.at[ssem], rsem.at[p], to[d])
 
     for p in range(NP):
-        mine, to = leg(p, 0)
-        for d in range(3):
-            send(mine, mine, s_send.at[8], hz_recv.at[p], to[d])
-
+        go(p, 0)
+    for p in range(NP):
+        go(p, 1)
+
+    mine = mbuf.at[0, c, unit(NU - 1)]
+    send(mine, mine, s_send.at[5], gc_recv.at[NU - 1], mate)
+    stage_g(NU - 2)
     stage_g(NU - 1)
     step = 64
 
@@ -288,9 +320,7 @@
         send(es.at[0], re.at[0, d], e_send.at[0], e_recv.at[0], zdev[d])
     for p in range(NP):
         wait(mbuf.at[0, 0, pl.ds(0, 2), 0, pl.ds(0, 3)], hz_recv.at[p])
-        mine, to = leg(p, 1)
-        for d in range(3):
-            send(mine, mine, s_send.at[9], hx_recv.at[p], to[d])
+        go(p, 2)
     wait(re.at[0], e_recv.at[0])
     es[1] = es[0] + re[0, 0] + re[0, 1] + re[0, 2]
     for d in range(3):
@@ -332,9 +362,11 @@
     wait(wall.at[pl.ds(0, 4)], w_send.at[0])
     wait(wall.at[0], w_send.at[1])
     wait(wall.at[pl.ds(0, 2)], w_send.at[2])
-    sizes = (rc, rx, rz, mbuf.at[0, 0, :, 0, pl.ds(0, 3)], mbuf.at[0, 0, :, pl.ds(0, 3)],
-             mbuf.at[0, 0], sg.at[0, :, pl.ds(0, 7)], sg.at[0],
-             mbuf.at[0, 0, :, 0, pl.ds(0, 3)], mbuf.at[0, 0, :, pl.ds(0, 3)], mbuf.at[0, 0])
+    most = pl.ds(0, NU - 1)
+    sizes = (rc, rx, rz, mbuf.at[0, 0, most, 0, pl.ds(0, 3)], mbuf.at[0, 0, most, pl.ds(0, 3)],
+             mbuf.at[0, 0], sg.at[0, :, pl.ds(0, 7)], sg.at[0, pl.ds(0, early)],
+             mbuf.at[0, 0, :, 0, pl.ds(0, 3)], mbuf.at[0, 0, :, pl.ds(0, 3)], mbuf.at[0, 0],
+             sg.at[0, pl.ds(0, 2)], fifteen)
     for k, ref in enumerate(sizes):
         wait(ref, s_send.at[k])
     wait(re.at[0], e_send.at[0])
@@ -385,7 +417,7 @@
             dma((NU,)),
             dma((NU,)),
             dma((CH,)),
-            dma((11,)),
+            dma((13,)),
             dma((NU,)),
             dma((NU,)),
             dma((NU,)),

time: 117 us -> 116 us (level)
  Pallas kernels: 115 us -> 113 us
    pallas_call x1, Pallas kernels: 115 us -> 113 us  [per_device(): pl.pallas_call(functools.partial(kernel, 2.0 * points / bands), out_shape...]
where the time goes in v4:
time: 116 us; the launch traced here: 115 us
  Pallas kernels  113 us (97%)
  local copies, waits for them, and re-layouts  1.54 us (1%)
    pallas_call x1, Pallas kernels, per_device(): pl.pallas_call(functools.partial(kernel, 2.0 * points / bands), out_shape...  113 us

profile of v4, /device:TPU:1, one launch (start us, length us, event | category | flops | bytes accessed | tf_op | source)
XLA Modules:
  0.0 115.5 jit_solution(12231845148566519987)
XLA Ops:
  0.6 113.3 %shard_map.41 = (bf16[256,2048]{1,0:T(8,128)(2,1)S(1)}, f32[2,128]{1,0:T(2,128)S(1)}) custom-call(bf16[256,2048]{1,0:T(8,128)(2,1)} %psi_hbm.1, bf16[256,2048]{1,0:T(8,128)(2,1)} %w_hbm.1), custom_call_target="tpu_custom_call" | custom-call | tf_op jit(solution)/shard_map/pallas_call | solution.py:385
  114.0 1.0 copy.6
  114.9 0.6 copy.7

commit v5 on v4

--- a/solution.py
+++ b/solution.py
@@ -180,6 +180,7 @@
         send(mine, mine, s_send.at[5], gc_recv.at[t], mate)
 
     width = 512
+    wide = 1024
 
     def stage_g(t):
         wait(mbuf.at[0, 0, 0], gc_recv.at[t])
@@ -215,6 +216,8 @@
 
         t = n - 1
 
+        over(stage_g, jnp.where(t == NU - 1, 0, 2), 2)
+
         @pl.when(t >= 0)
         def _():
             wait(wall.at[0, 0], m_recv.at[t])
@@ -236,11 +239,9 @@
         return carry
 
     lax.fori_loop(0, NU + 1, tick, 0)
-    stage_g(0)
     stage_c(NU - 1)
     stage_e(NU - 3)
     stage_f(NU - 4)
-    stage_g(1)
     stage_d(NU - 2)
     spread(NU - 2)
     stage_g(2)
@@ -345,13 +346,13 @@
         turn(p, 1 - c)
 
     def last(i, carry):
-        at = pl.ds(pl.multiple_of(i * width, width), width)
-        change = jnp.dot(mt2[...], wall[:, :, :, at].reshape(NU * rows, width),
+        at = pl.ds(pl.multiple_of(i * wide, wide), wide)
+        change = jnp.dot(mt2[...], wall[:, :, :, at].reshape(NU * rows, wide),
                          preferred_element_type=F32)
         res[:, at] = (psi1[:, at].astype(F32) - change).astype(BF16)
         return carry
 
-    lax.fori_loop(0, cols // width, last, 0)
+    lax.fori_loop(0, cols // wide, last, 0)
 
     wait(re.at[2, 0], e_recv.at[2])
     mine, other = es[2, 0:1, :], re[2, 0, 0:1, :]

time: 116 us -> 115 us (level)
  no operation moved by 1% of the time
where the time goes in v5:
time: 115 us
  Pallas kernels  113 us (98%)
  local copies, waits for them, and re-layouts  1.54 us (1%)
    pallas_call x1, Pallas kernels, per_device(): pl.pallas_call(functools.partial(kernel, 2.0 * points / bands), out_shape...  113 us

profile of v5, /device:TPU:1, one launch (start us, length us, event | category | flops | bytes accessed | tf_op | source)
XLA Modules:
  0.0 115.1 jit_solution(13268131928279130914)
XLA Ops:
  0.6 112.9 %shard_map.41 = (bf16[256,2048]{1,0:T(8,128)(2,1)S(1)}, f32[2,128]{1,0:T(2,128)S(1)}) custom-call(bf16[256,2048]{1,0:T(8,128)(2,1)} %psi_hbm.1, bf16[256,2048]{1,0:T(8,128)(2,1)} %w_hbm.1), custom_call_target="tpu_custom_call" | custom-call | tf_op jit(solution)/shard_map/pallas_call | solution.py:386
  113.6 1.0 copy.6
  114.5 0.6 copy.7
